TPU v7x, 32 devices: a whole 2x2x4 slice. The times are simulated.
32 devices in a mesh: rep: 4 (over y, x), ep: 8 (over z, core).
Axes of the slice: x: 2, y: 2, z: 4, core: 2. Of those that a mesh axis runs over, the one named last changes fastest.
Arguments:
- out_grad: bfloat16 [2048, 2048], P(('rep', 'ep')), may hold values from -3 to 3
- saved_hidden: bfloat16 [2048, 2, 7168], P(('rep', 'ep')), may hold values from -0.59765625 to 0.59765625
- combine: bfloat16 [2048, 2], P(('rep', 'ep')), may hold values from 0.049804688 to 1
- expert_ids: int32 [2048, 2], P(('rep', 'ep')), may hold values from 0 to 7, all different within a row; in each aligned block of 64 rows (0 to 63, 64 to 127, ...) at most 24 rows name the same one
Outputs:
- down_grad: float32 [57344, 2048], P('ep', 'rep')
Inputs may be any that keep to these rules, and one draw needn't show every extreme that they name: `expert_ids`: in each aligned block of 64 rows (the rows of one device), no expert is named by more than 24 slots, a bound that some block reaches; the 2 ids of a row differ; every expert is named somewhere.
All inputs are finite; a program needn't handle non-finite values.
Results may differ from a plain program's by a relative error of at most 0.0042.
Values may be sent and summed in bfloat16 or wider, within the bound.
A program may use at most 64 MiB of HBM per device.

v0:
```python
import jax
import jax.numpy as jnp
from jax import lax
from jax.sharding import PartitionSpec as P

EXPERTS = 8
TOP = 2
CAP = 24


def per_device(out_grad, saved_hidden, combine, expert_ids):
    ep_count = lax.axis_size("ep")
    rep_count = lax.axis_size("rep")
    group_size = ep_count // EXPERTS
    tok_count = out_grad.shape[0]
    slot_count = tok_count * TOP
    unit_cols = saved_hidden.shape[2] // group_size
    model_width = out_grad.shape[1]
    flat_ids = expert_ids.reshape(slot_count)
    onehot = (flat_ids[:, None] == jnp.arange(EXPERTS, dtype=jnp.int32)[None, :]).astype(jnp.int32)
    slot_place = jnp.sum((jnp.cumsum(onehot, axis=0) - 1) * onehot, axis=1)
    slot_grad = jnp.broadcast_to(out_grad[:, None, :], (tok_count, TOP, model_width)).reshape(
        slot_count, model_width
    )
    send_grad = (
        jnp.zeros((EXPERTS, CAP, model_width), jnp.bfloat16).at[flat_ids, slot_place].set(slot_grad)
    )
    send_grad = jnp.broadcast_to(
        send_grad[:, None], (EXPERTS, group_size, CAP, model_width)
    ).reshape(ep_count, CAP, model_width)
    hidden_pieces = saved_hidden.reshape(slot_count, group_size, unit_cols)
    send_hidden = (
        jnp.zeros((EXPERTS, group_size, CAP, unit_cols), jnp.bfloat16)
        .at[flat_ids, :, slot_place, :]
        .set(hidden_pieces)
    )
    slot_prob = jnp.broadcast_to(combine.reshape(slot_count)[:, None], (slot_count, group_size))
    send_prob = (
        jnp.zeros((EXPERTS, group_size, CAP), jnp.bfloat16)
        .at[flat_ids, :, slot_place]
        .set(slot_prob)
    )
    recv_grad, recv_hidden, recv_prob = (
        lax.all_to_all(send_grad, "ep", split_axis=0, concat_axis=0, tiled=True),
        lax.all_to_all(
            send_hidden.reshape(ep_count, CAP, unit_cols),
            "ep",
            split_axis=0,
            concat_axis=0,
            tiled=True,
        ),
        lax.all_to_all(
            send_prob.reshape(ep_count, CAP), "ep", split_axis=0, concat_axis=0, tiled=True
        ),
    )
    row_total = ep_count * CAP
    grad_rows = recv_grad.reshape(row_total, model_width)
    hidden_rows = recv_hidden.reshape(row_total, unit_cols)
    prob_rows = recv_prob.reshape(row_total)
    scaled_all = (prob_rows[:, None].astype(jnp.float32) * grad_rows.astype(jnp.float32)).astype(
        jnp.bfloat16
    )
    contract_rows = (((0,), (0,)), ((), ()))
    col_width = model_width // rep_count
    spread_cols = lax.all_to_all(
        scaled_all.reshape(row_total, rep_count, col_width),
        "rep",
        split_axis=1,
        concat_axis=0,
        tiled=True,
    )
    spread_cols = spread_cols.reshape(rep_count * row_total, col_width)
    return lax.dot_general(
        lax.all_gather(hidden_rows, "rep", axis=0, tiled=True),
        spread_cols,
        contract_rows,
        preferred_element_type=jnp.float32,
    )


def solution(mesh):
    in_specs = (
        P(("rep", "ep"), None),
        P(("rep", "ep"), None, None),
        P(("rep", "ep"), None),
        P(("rep", "ep"), None),
    )
    out_specs = P("ep", "rep")
    return jax.shard_map(
        per_device, mesh=mesh, in_specs=in_specs, out_specs=out_specs, check_vma=False
    )
```

profile of v0, /device:TPU:8, one launch (start us, length us, event | category | flops | bytes accessed | tf_op | source)
XLA Modules:
  0.0 256.3 jit_solution(115714935663916148)
XLA Ops:
  6.5 0.0 all-gather.2.cloned.1.call-start
  6.5 0.8 copy.15
  7.3 0.1 eq.15
  7.4 0.1 reshape.86
  7.6 0.1 fusion
  7.7 0.2 reduce_window_sum.11
  7.9 0.2 select_reduce_fusion
  8.0 4.9 %reshape.100 = bf16[128,7168]{1,0:T(8,128)(2,1)} reshape(bf16[64,2,7168]{2,1,0:T(2,128)(2,1)} %param.5) | data formatting | bytes 3670016 | tf_op jit(solution)/shard_map/reshape | solution.py:31
  13.0 0.3 broadcast.101
  13.3 38.2 %scatter_fusion = bf16[8,24,7168]{2,1,0:T(8,128)(2,1)S(1)} fusion(bf16[8,24,7168]{2,1,0:T(8,128)(2,1)S(1)} %broadcast.101, s32[128]{0:T(128)S(1)} %fusion.2, bf16[128,7168]{1,0:T(8,128)(2,1)} %reshape.100), kind=kCustom, calls=%fused_computation | custom fusion | bytes 5506048 | tf_op jit(solution)/shard_map/scatter | solution.py:35
  51.5 66.5 %all_to_all.31 = bf16[8,24,7168]{2,1,0:T(8,128)(2,1)} all-to-all(bf16[8,24,7168]{2,1,0:T(8,128)(2,1)S(1)} %scatter_fusion), channel_id=1, replica_groups=mesh['rep'=4,'ep'=8] {'ep'}, dimensions={0} | all-to-all | bytes 5505024 | tf_op jit(solution)/shard_map/all_to_all | solution.py:45
  118.0 0.0 copy-start.1
  118.0 0.0 copy-start
  118.0 0.0 all-gather.2.cloned.1.call-update
  118.0 0.6 copy-done.1
  118.7 0.1 copy.17
  118.8 0.1 reshape.110
  118.9 6.5 %scatter_fusion.1 = bf16[8,24]{1,0:T(8,128)(2,1)S(1)} fusion(bf16[8,24]{1,0:T(8,128)(2,1)S(1)} %broadcast.103, s32[128]{0:T(128)S(1)} %fusion.2, bf16[128]{0:T(256)(128)(2,1)S(1)} %reshape.110), kind=kCustom, calls=%fused_computation.1 | custom fusion | bytes 1792 | tf_op jit(solution)/shard_map/scatter | solution.py:41
  125.5 0.6 copy.18
  126.0 5.0 %all-to-all-start.1 = ((bf16[8,1,24]{2,1,0:T(2,128)(2,1)}), bf16[8,1,24]{2,1,0:T(2,128)(2,1)S(1)}, u32[]{:S(2)}, u32[]{:S(2)}) async-start(bf16[8,1,24]{2,1,0:T(2,128)(2,1)} %copy.18), calls=%async_computation.1 | async-start | bytes 8192 | tf_op jit(solution)/shard_map/all_to_all | solution.py:52
  131.0 0.0 copy-done
  131.0 0.3 broadcast_in_dim.11
  131.4 0.2 reshape.116
  131.6 1.0 broadcast_in_dim.10
  132.5 23.0 %scatter_fusion.2 = bf16[8,24,2048]{2,1,0:T(8,128)(2,1)} fusion(bf16[8,24,2048]{2,1,0:T(8,128)(2,1)} %broadcast_in_dim.10, s32[128]{0:T(128)S(1)} %fusion.2, bf16[128,2048]{1,0:T(8,128)(2,1)S(1)} %reshape.116), kind=kCustom, calls=%fused_computation.2 | custom fusion | bytes 1573888 | tf_op jit(solution)/shard_map/scatter | solution.py:26
  155.6 0.0 all-to-all-done.1
  155.6 5.3 %all-to-all-start.2 = ((bf16[8,24,2048]{2,1,0:T(8,128)(2,1)}), bf16[8,24,2048]{2,1,0:T(8,128)(2,1)S(1)}, u32[]{:S(2)}, u32[]{:S(2)}) async-start(bf16[8,24,2048]{2,1,0:T(8,128)(2,1)} %scatter_fusion.2), calls=%async_computation.2 | async-start | bytes 1572864 | tf_op jit(solution)/shard_map/all_to_all | solution.py:44
  160.9 0.1 reshape.92
  160.9 17.4 %all-to-all-done.2 = bf16[8,24,2048]{2,1,0:T(8,128)(2,1)S(1)} async-done(((bf16[8,24,2048]{2,1,0:T(8,128)(2,1)}), bf16[8,24,2048]{2,1,0:T(8,128)(2,1)S(1)}, u32[]{:S(2)}, u32[]{:S(2)}) %all-to-all-start.2) | async-done | bytes 786464 | tf_op jit(solution)/shard_map/all_to_all | solution.py:44
  178.4 1.2 reshape.93
  179.6 0.3 multiply_convert_fusion
  180.0 0.1 copy.19
  180.1 23.9 %all_to_all.32 = bf16[192,4,512]{2,0,1:T(8,128)(2,1)S(1)} all-to-all(bf16[192,4,512]{2,0,1:T(8,128)(2,1)S(1)} %copy.19), channel_id=1, replica_groups=mesh['rep'=4,'ep'=8] {'rep'}, dimensions={1} | all-to-all | bytes 1572864 | tf_op jit(solution)/shard_map/all_to_all | solution.py:65
  204.0 32.1 %all-gather.2.cloned.1.call-done = bf16[768,7168]{1,0:T(8,128)(2,1)} async-done(((bf16[192,7168]{1,0:T(8,128)(2,1)}), bf16[768,7168]{1,0:T(8,128)(2,1)}) %all-gather.2.cloned.1.call-update) | async-done | bytes 11010064 | tf_op jit(solution)/shard_map/all_gather | solution.py:74
  236.1 13.3 %fusion.3 = f32[7168,512]{1,0:T(8,128)} fusion(bf16[768,7168]{1,0:T(8,128)(2,1)} %all-gather.2.cloned.1.call-done, bf16[768,512]{1,0:T(8,128)(2,1)S(1)} %bitcast.20), kind=kOutput, calls=%fused_computation.15 | convolution fusion | flops 5637144576 | bytes 26476544 | tf_op jit(solution)/shard_map/dot_general | solution.py:73
  (3 shorter events, 0.0 us)
Async XLA Ops:
  6.5 229.6 %all-gather.2.cloned.1.call-start = ((), (), s32[]{:S(2)}) async-start(), calls=%async_computation.4 | async-start | bytes 13762560 | tf_op jit(solution)/shard_map/all_gather | solution.py:74
  118.0 0.7 copy-start.1
  118.0 13.0 %copy-start = (bf16[64,2048]{1,0:T(8,128)(2,1)S(1)}, bf16[64,2048]{1,0:T(8,128)(2,1)}, u32[]{:S(2)}) copy-start(bf16[64,2048]{1,0:T(8,128)(2,1)} %param.4) | copy-start | bytes 786436
  126.0 29.5 %all-to-all-start.1 = ((bf16[8,1,24]{2,1,0:T(2,128)(2,1)}), bf16[8,1,24]{2,1,0:T(2,128)(2,1)S(1)}, u32[]{:S(2)}, u32[]{:S(2)}) async-start(bf16[8,1,24]{2,1,0:T(2,128)(2,1)} %copy.18), calls=%async_computation.1 | async-start | bytes 8192 | tf_op jit(solution)/shard_map/all_to_all | solution.py:52
  155.6 22.8 %all-to-all-start.2 = ((bf16[8,24,2048]{2,1,0:T(8,128)(2,1)}), bf16[8,24,2048]{2,1,0:T(8,128)(2,1)S(1)}, u32[]{:S(2)}, u32[]{:S(2)}) async-start(bf16[8,24,2048]{2,1,0:T(8,128)(2,1)} %scatter_fusion.2), calls=%async_computation.2 | async-start | bytes 1572864 | tf_op jit(solution)/shard_map/all_to_all | solution.py:44
Sparse Core Ops, SparseCore 0:
  118.2 117.9 all-gather.1
where the time goes:
time: 259 us; the launch traced here: 256 us
  blocking collectives  90.4 us (35%)
  local copies, waits for them, and re-layouts  78.4 us (30%)
  waiting for transfers between devices  49.5 us (19%)
  between operations  13.5 us (5%)
  matrix products  13.3 us (5%)
  starting transfers between devices  10.3 us (4%)
    all_to_all x1, blocking collectives, per_device(): lax.all_to_all(send_hidden.reshape(ep_count, CAP, unit_cols), 'ep', split...  66.5 us
    scatter x1, local copies, waits for them, and re-layouts, per_device(): send_hidden = jnp.zeros((EXPERTS, group_size, CAP, unit_cols), jnp.bfloat...  38.2 us
    all_gather x1, waiting for transfers between devices, per_device(): lax.all_gather(hidden_rows, 'rep', axis=0, tiled=True)  32.1 us
    all_to_all x1, blocking collectives, per_device(): lax.all_to_all(scaled_all.reshape(row_total, rep_count, col_width), 'rep'...  23.9 us
    scatter x1, local copies, waits for them, and re-layouts, per_device(): jnp.zeros((EXPERTS, CAP, model_width), jnp.bfloat16)  23 us
    all_to_all x1, waiting for transfers between devices, per_device(): lax.all_to_all(send_grad, 'ep', split_axis=0, concat_axis=0, tiled=True)  17.4 us
    dot_general x1, matrix products, per_device(): lax.dot_general(lax.all_gather(hidden_rows, 'rep', axis=0, tiled=True), s...  13.3 us
    scatter x2, local copies, waits for them, and re-layouts, per_device(): send_prob = jnp.zeros((EXPERTS, group_size, CAP), jnp.bfloat16).at[flat_i...  7.09 us
  transfers between devices with their start and end apart: 3, of which 2 were waited for; matrix products, arithmetic and copies ran while one was open for 13% of the time, Pallas kernels for 0%

commit v1 on v0

v1 whole, which is shorter than its diff:
```python
import functools

import jax
import jax.numpy as jnp
from jax import lax
from jax.experimental import pallas as pl
from jax.experimental.pallas import tpu as pltpu
from jax.sharding import PartitionSpec as P

EXPERTS = 8
TOP = 2
CAP = 24
MESH = pl.DeviceIdType.MESH


def xor(place, pattern):
    bit = 1
    while bit <= pattern:
        if pattern & bit:
            place = place + bit - 2 * bit * ((place // bit) % 2)
        bit *= 2
    return place


def partners(ep_count):
    pairs = ep_count // 2
    if ep_count & (ep_count - 1) == 0 and pairs >= 2:
        chips = [pairs - 1] + list(range(1, pairs - 1))
        order = [0, 1] + [2 * chip + core for chip in chips for core in (0, 1)]
        return [(lambda p, k=k: xor(p, k), lambda p, k=k: xor(p, k)) for k in order]
    return [
        (lambda p, k=k: (p + k) % ep_count, lambda p, k=k: (p + ep_count - k) % ep_count)
        for k in range(ep_count)
    ]


def ring_place(rep_count):
    if rep_count == 4:
        swap = lambda q: q + q // 2 - 2 * (q // 3)
        return swap, swap
    return (lambda q: q), (lambda q: q)


def exchange_kernel(
    rep_count, ep_count, hidden_ref, grad_ref, rows_ref, cols_ref,
    own_sem, send_sem, recv_sem, ring_send, ring_recv, grad_send, grad_recv,
):
    rep, ep = lax.axis_index("rep"), lax.axis_index("ep")
    group = ep_count // EXPERTS
    unit_cols = rows_ref.shape[3]
    col_width = cols_ref.shape[3]
    to_ring, from_ring = ring_place(rep_count)
    place = to_ring(rep)
    at = lambda off: from_ring((place + off + rep_count) % rep_count)
    steps = partners(ep_count)
    full_hops = (rep_count - 1) // 2
    half_hop = rep_count % 2 == 0
    half = unit_cols // 2 // 128 * 128
    parts = {0: pl.ds(0, half), 1: pl.ds(half, unit_cols - half)}

    def piece_for(dest):
        start = pl.multiple_of((dest % group) * unit_cols, 128)
        return hidden_ref.at[dest // group, :, pl.ds(start, unit_cols)]

    def remote(src, dst, send, recv, to_rep, to_ep):
        return pltpu.make_async_remote_copy(
            src_ref=src, dst_ref=dst, send_sem=send, recv_sem=recv,
            device_id=(to_rep, to_ep), device_id_type=MESH,
        )

    started = []
    own = pltpu.make_async_copy(piece_for(ep), rows_ref.at[rep, ep], own_sem.at[0])
    own_cols = pltpu.make_async_copy(
        grad_ref.at[ep // group, :, pl.ds(pl.multiple_of(rep * col_width, 128), col_width)],
        cols_ref.at[rep, ep], own_sem.at[1],
    )

    exchanges = [None]
    for i in range(1, ep_count):
        dest = steps[i][0](ep)
        exchanges.append(
            remote(piece_for(dest), rows_ref.at[rep, ep], send_sem.at[i], recv_sem.at[i], rep, dest)
        )

    def hop(i, way, distance):
        source = steps[i][1](ep)
        origin = at(-way * (distance - 1))
        src = rows_ref.at[origin, source]
        dst = rows_ref.at[origin, source]
        if distance == 1 and i == 0:
            src = piece_for(ep)
        if distance > full_hops:
            cut = parts[0 if way == 1 else 1]
            src, dst = src.at[:, cut], dst.at[:, cut]
        lane = (0 if way == 1 else 1, distance - 1, i)
        return remote(src, dst, ring_send.at[lane], ring_recv.at[lane], at(way), ep)

    last_hop = full_hops + (1 if half_hop else 0)
    grads = []

    def send_grads():
        for r in range(rep_count):
            for i in range(ep_count):
                if r == 0 and i == 0:
                    continue
                to_rep, to_ep = at(r), steps[i][0](ep)
                start = pl.multiple_of(to_rep * col_width, 128)
                copy = remote(
                    grad_ref.at[to_ep // group, :, pl.ds(start, col_width)],
                    cols_ref.at[rep, ep], grad_send.at[r, i], grad_recv.at[r, i], to_rep, to_ep,
                )
                copy.start()
                grads.append(copy)

    for copy in exchanges[1:2]:
        copy.start()
    hops = {}

    def start_hop(i, distance):
        if distance > last_hop:
            return
        for way in (1, -1):
            hops[i, way, distance] = hop(i, way, distance)
            hops[i, way, distance].start()

    start_hop(0, 1)
    for copy in exchanges[2:]:
        copy.start()
    own.start()
    own_cols.start()
    for i in range(1, ep_count + last_hop):
        if i < ep_count:
            exchanges[i].wait_recv()
            start_hop(i, 1)
        if i == 1:
            send_grads()
        for distance in range(1, last_hop + 1):
            j = i - distance
            if 0 <= j < ep_count:
                for way in (1, -1):
                    hops[j, way, distance].wait_recv()
                start_hop(j, distance + 1)
    for copy in grads:
        copy.wait()
    for copy in exchanges[1:]:
        copy.wait_send()
    for copy in hops.values():
        copy.wait_send()
    own.wait()
    own_cols.wait()


def exchange(hidden, grad, rep_count, ep_count):
    unit_cols = hidden.shape[2] * EXPERTS // ep_count
    col_width = grad.shape[2] // rep_count
    hops = max(1, rep_count // 2)
    return pl.pallas_call(
        functools.partial(exchange_kernel, rep_count, ep_count),
        out_shape=(
            jax.ShapeDtypeStruct((rep_count, ep_count, CAP, unit_cols), jnp.bfloat16),
            jax.ShapeDtypeStruct((rep_count, ep_count, CAP, col_width), jnp.bfloat16),
        ),
        in_specs=[pl.BlockSpec(memory_space=pl.ANY)] * 2,
        out_specs=(pl.BlockSpec(memory_space=pl.ANY),) * 2,
        scratch_shapes=[
            pltpu.SemaphoreType.DMA((2,)),
            pltpu.SemaphoreType.DMA((ep_count,)),
            pltpu.SemaphoreType.DMA((ep_count,)),
            pltpu.SemaphoreType.DMA((2, hops, ep_count)),
            pltpu.SemaphoreType.DMA((2, hops, ep_count)),
            pltpu.SemaphoreType.DMA((rep_count, ep_count)),
            pltpu.SemaphoreType.DMA((rep_count, ep_count)),
        ],
        compiler_params=pltpu.CompilerParams(has_side_effects=True),
    )(hidden, grad)


def per_device(out_grad, saved_hidden, combine, expert_ids):
    ep_count = lax.axis_size("ep")
    rep_count = lax.axis_size("rep")
    tok_count, model_width = out_grad.shape
    slot_count = tok_count * TOP
    units = saved_hidden.shape[2]
    flat_ids = expert_ids.reshape(slot_count)
    onehot = (flat_ids[:, None] == jnp.arange(EXPERTS, dtype=jnp.int32)[None, :]).astype(jnp.int32)
    slot_place = jnp.sum((jnp.cumsum(onehot, axis=0) - 1) * onehot, axis=1)
    row_of_slot = (flat_ids * CAP + slot_place).reshape(tok_count, TOP)
    packed = jnp.arange(EXPERTS * CAP, dtype=jnp.int32)
    pick = packed[:, None, None] == row_of_slot[None]
    pick_token = jnp.any(pick, axis=2).astype(jnp.bfloat16)
    packed_prob = jnp.sum(
        jnp.where(pick, combine[None].astype(jnp.float32), jnp.float32(0.0)), axis=(1, 2)
    )
    send_hidden = lax.dot_general(
        pick.astype(jnp.bfloat16).reshape(EXPERTS * CAP, slot_count),
        saved_hidden.reshape(slot_count, units),
        (((1,), (0,)), ((), ())),
        preferred_element_type=jnp.float32,
    ).astype(jnp.bfloat16)
    grad_rows = jnp.dot(pick_token, out_grad, preferred_element_type=jnp.float32)
    send_grad = (packed_prob[:, None] * grad_rows).astype(jnp.bfloat16)
    rows, cols = exchange(
        send_hidden.reshape(EXPERTS, CAP, units),
        send_grad.reshape(EXPERTS, CAP, model_width),
        rep_count,
        ep_count,
    )
    row_total = rep_count * ep_count * CAP
    return lax.dot_general(
        rows.reshape(row_total, rows.shape[3]),
        cols.reshape(row_total, cols.shape[3]),
        (((0,), (0,)), ((), ())),
        preferred_element_type=jnp.float32,
    )


def solution(mesh):
    in_specs = (
        P(("rep", "ep"), None),
        P(("rep", "ep"), None, None),
        P(("rep", "ep"), None),
        P(("rep", "ep"), None),
    )
    out_specs = P("ep", "rep")
    return jax.shard_map(
        per_device, mesh=mesh, in_specs=in_specs, out_specs=out_specs, check_vma=False
    )
```

time: 259 us -> 131 us (0.51)
  Pallas kernels: 0 us -> 111 us
  blocking collectives: 90.4 us -> 0 us
  local copies, waits for them, and re-layouts: 78.4 us -> 1.12 us
  waiting for transfers between devices: 49.5 us -> 0 us
  between operations: 13.5 us -> 0.05 us
  starting transfers between devices: 10.3 us -> 0 us
  matrix products: 13.3 us -> 16.7 us
    pallas_call x0 -> x1, Pallas kernels: none -> 111 us  [exchange(): pl.pallas_call(functools.partial(exchange_kernel, rep_count, ep_count), o...]
    all_to_all x2 -> x0, blocking collectives: 90.4 us -> none  [the longest x1 66.5 us: per_device(): lax.all_to_all(send_hidden.reshape(ep_count, CAP, unit_cols), 'ep', split...]
    scatter x4 -> x0, local copies, waits for them, and re-layouts: 68.4 us -> none  [the longest x1 38.2 us: per_device(): send_hidden = jnp.zeros((EXPERTS, group_size, CAP, unit_cols), jnp.bfloat...]
    all_gather x1 -> x0, waiting for transfers between devices: 32.1 us -> none  [per_device(): lax.all_gather(hidden_rows, 'rep', axis=0, tiled=True)]
    all_to_all x2 -> x0, waiting for transfers between devices: 17.4 us -> none  [the longest x1 17.4 us: per_device(): lax.all_to_all(send_grad, 'ep', split_axis=0, concat_axis=0, tiled=True)]
    all_to_all x2 -> x0, starting transfers between devices: 10.3 us -> none  [the longest x1 5.28 us: per_device(): lax.all_to_all(send_grad, 'ep', split_axis=0, concat_axis=0, tiled=True)]
    reshape x3 -> x0, local copies, waits for them, and re-layouts: 5.26 us -> none  [the longest x1 4.92 us: per_device(): hidden_pieces = saved_hidden.reshape(slot_count, group_size, unit_cols)]
    dot_general x1 -> x3, matrix products: 13.3 us -> 16.7 us  [the longest x1 11.9 us: per_device(): lax.dot_general(rows.reshape(row_total, rows.shape[3]), cols.reshape(row_...]
  transfers between devices with their start and end apart: 3 -> 0, of which waited for: 2 -> 0; matrix products, arithmetic and copies ran while one was open for 13% -> 0% of each run, Pallas kernels for 0% -> 0%
where the time goes in v1:
time: 131 us
  Pallas kernels  111 us (85%)
  matrix products  16.7 us (13%)
  other arithmetic  2.12 us (2%)
    pallas_call x1, Pallas kernels, exchange(): pl.pallas_call(functools.partial(exchange_kernel, rep_count, ep_count), o...  111 us
    dot_general x1, matrix products, per_device(): lax.dot_general(rows.reshape(row_total, rows.shape[3]), cols.reshape(row_...  11.9 us

profile of v1, /device:TPU:8, one launch (start us, length us, event | category | flops | bytes accessed | tf_op | source)
XLA Modules:
  0.0 130.8 jit_solution(2468059321147642925)
XLA Ops:
  0.0 0.0 copy-start
  0.0 0.8 convert_element_type.17
  0.8 0.8 copy.20
  1.6 0.1 eq.29
  1.7 0.1 fusion.5
  1.8 0.2 reduce_window_sum.11
  2.0 0.2 select_reduce_fusion.1
  2.1 0.1 reduce_sum.21
  2.3 0.1 copy.21
  2.4 0.7 multiply_add_fusion
  3.1 0.1 select_reduce_fusion
  3.2 0.1 fusion.3
  3.3 2.3 %fusion.1 = bf16[192,2048]{1,0:T(8,128)(2,1)} fusion(pred[192,64]{0,1:T(8,128)(4,1)S(1)} %fusion.3, bf16[64,2048]{1,0:T(8,128)(2,1)} %param.4, f32[192]{0:T(256)S(1)} %select_reduce_fusion), kind=kOutput, calls=%fused_computation.4 | convolution fusion | flops 51118080 | bytes 1061632 | tf_op jit(solution)/shard_map/dot_general | solution.py:200
  5.5 0.0 copy-done
  5.5 2.5 %fusion = bf16[192,7168]{1,0:T(8,128)(2,1)} fusion(bf16[64,2,7168]{2,1,0:T(2,128)(2,1)S(1)} %copy-done, s32[64,2]{0,1:T(2,128)S(1)} %multiply_add_fusion), kind=kOutput, calls=%fused_computation.2 | convolution fusion | flops 353722368 | bytes 4588032 | tf_op jit(solution)/shard_map/dot_general | solution.py:194
  8.1 110.8 %shard_map.46 = (bf16[4,8,24,7168]{3,2,1,0:T(8,128)(2,1)}, bf16[4,8,24,512]{3,2,1,0:T(8,128)(2,1)}) custom-call(bf16[8,24,7168]{2,1,0:T(8,128)(2,1)} %bitcast.14, bf16[8,24,2048]{2,1,0:T(8,128)(2,1)} %bitcast.15), custom_call_target="tpu_custom_call" | custom-call | tf_op jit(solution)/shard_map/pallas_call | solution.py:157
  118.9 11.9 %convolution_bitcast_fusion = f32[7168,512]{1,0:T(8,128)} fusion(bf16[4,8,24,7168]{3,2,1,0:T(8,128)(2,1)} %get-tuple-element.7, bf16[4,8,24,512]{3,2,1,0:T(8,128)(2,1)} %get-tuple-element.8), kind=kOutput, calls=%fused_computation | convolution fusion | flops 5637144576 | bytes 26476544 | tf_op jit(solution)/shard_map/dot_general | solution.py:209
Async XLA Ops:
  0.0 5.5 %copy-start = (bf16[64,2,7168]{2,1,0:T(2,128)(2,1)S(1)}, bf16[64,2,7168]{2,1,0:T(2,128)(2,1)}, u32[]{:S(2)}) copy-start(bf16[64,2,7168]{2,1,0:T(2,128)(2,1)} %param.5) | copy-start | bytes 5505028

commit v2 on v1

--- a/solution.py
+++ b/solution.py
@@ -171,7 +171,7 @@
             pltpu.SemaphoreType.DMA((rep_count, ep_count)),
             pltpu.SemaphoreType.DMA((rep_count, ep_count)),
         ],
-        compiler_params=pltpu.CompilerParams(has_side_effects=True),
+        compiler_params=pltpu.CompilerParams(has_side_effects=True, vmem_limit_bytes=1024 * 1024),
     )(hidden, grad)
 
 

time: 131 us -> 125 us (0.954)
  matrix products: 16.7 us -> 11.8 us
    dot_general x1, matrix products: 11.9 us -> 9.45 us  [per_device(): lax.dot_general(rows.reshape(row_total, rows.shape[3]), cols.reshape(row_...]
    dot_general x1, matrix products: 2.52 us -> 0.98 us  [per_device(): lax.dot_general(pick.astype(jnp.bfloat16).reshape(EXPERTS * CAP, slot_cou...]
where the time goes in v2:
time: 125 us
  Pallas kernels  110 us (88%)
  matrix products  11.8 us (9%)
  other arithmetic  2.12 us (2%)
    pallas_call x1, Pallas kernels, exchange(): pl.pallas_call(functools.partial(exchange_kernel, rep_count, ep_count), o...  110 us
    dot_general x1, matrix products, per_device(): lax.dot_general(rows.reshape(row_total, rows.shape[3]), cols.reshape(row_...  9.45 us

profile of v2, /device:TPU:8, one launch (start us, length us, event | category | flops | bytes accessed | tf_op | source)
XLA Modules:
  0.0 125.3 jit_solution(8396196896015747590)
XLA Ops:
  0.0 0.0 copy-start
  0.0 0.8 convert_element_type.17
  0.8 0.8 copy.20
  1.6 0.1 eq.29
  1.7 0.1 fusion.5
  1.8 0.2 reduce_window_sum.11
  2.0 0.2 select_reduce_fusion.1
  2.1 0.1 reduce_sum.21
  2.3 0.1 copy.21
  2.4 0.7 multiply_add_fusion
  3.1 0.1 select_reduce_fusion
  3.2 0.1 fusion.3
  3.3 1.4 %fusion.1 = bf16[192,2048]{1,0:T(8,128)(2,1)S(1)} fusion(pred[192,64]{0,1:T(8,128)(4,1)S(1)} %fusion.3, bf16[64,2048]{1,0:T(8,128)(2,1)} %param.4, f32[192]{0:T(256)S(1)} %select_reduce_fusion), kind=kOutput, calls=%fused_computation.4 | convolution fusion | flops 51118080 | bytes 1061632 | tf_op jit(solution)/shard_map/dot_general | solution.py:200
  4.6 0.0 copy-done
  4.6 1.0 fusion
  5.6 110.2 %shard_map.46 = (bf16[4,8,24,7168]{3,2,1,0:T(8,128)(2,1)S(1)}, bf16[4,8,24,512]{3,2,1,0:T(8,128)(2,1)S(1)}) custom-call(bf16[8,24,7168]{2,1,0:T(8,128)(2,1)S(1)} %bitcast.14, bf16[8,24,2048]{2,1,0:T(8,128)(2,1)S(1)} %bitcast.15), custom_call_target="tpu_custom_call" | custom-call | tf_op jit(solution)/shard_map/pallas_call | solution.py:157
  115.9 9.4 %convolution_bitcast_fusion = f32[7168,512]{1,0:T(8,128)} fusion(bf16[4,8,24,7168]{3,2,1,0:T(8,128)(2,1)S(1)} %get-tuple-element.7, bf16[4,8,24,512]{3,2,1,0:T(8,128)(2,1)S(1)} %get-tuple-element.8), kind=kOutput, calls=%fused_computation | convolution fusion | flops 5637144576 | bytes 26476544 | tf_op jit(solution)/shard_map/dot_general | solution.py:209
Async XLA Ops:
  0.0 4.6 %copy-start = (bf16[64,2,7168]{2,1,0:T(2,128)(2,1)S(1)}, bf16[64,2,7168]{2,1,0:T(2,128)(2,1)}, u32[]{:S(2)}) copy-start(bf16[64,2,7168]{2,1,0:T(2,128)(2,1)} %param.5) | copy-start | bytes 5505028

commit v3 on v2

v3 whole, which is shorter than its diff:
```python
import functools

import jax
import jax.numpy as jnp
from jax import lax
from jax.experimental import pallas as pl
from jax.experimental.pallas import tpu as pltpu
from jax.sharding import PartitionSpec as P

EXPERTS = 8
TOP = 2
CAP = 24
MESH = pl.DeviceIdType.MESH


def xor(place, pattern):
    bit = 1
    while bit <= pattern:
        if pattern & bit:
            place = place + bit - 2 * bit * ((place // bit) % 2)
        bit *= 2
    return place


def partners(ep_count):
    pairs = ep_count // 2
    if ep_count & (ep_count - 1) == 0 and pairs >= 2:
        chips = [pairs - 1] + list(range(1, pairs - 1))
        order = [0, 1] + [2 * chip + core for chip in chips for core in (0, 1)]
        return [(lambda p, k=k: xor(p, k), lambda p, k=k: xor(p, k)) for k in order]
    return [
        (lambda p, k=k: (p + k) % ep_count, lambda p, k=k: (p + ep_count - k) % ep_count)
        for k in range(ep_count)
    ]


def ring_place(rep_count):
    if rep_count == 4:
        swap = lambda q: q + q // 2 - 2 * (q // 3)
        return swap, swap
    return (lambda q: q), (lambda q: q)


def exchange_kernel(
    rep_count, ep_count, hidden_ref, grad_ref, route_ref, rows_ref, cols_ref,
    grads, routes, packed, own_sem, send_sem, recv_sem, ring_send, ring_recv,
    grad_send, grad_recv, route_send, route_recv, cols_send, cols_recv,
):
    rep, ep = lax.axis_index("rep"), lax.axis_index("ep")
    group = ep_count // EXPERTS
    unit_cols = rows_ref.shape[3]
    col_width = cols_ref.shape[3]
    to_ring, from_ring = ring_place(rep_count)
    place = to_ring(rep)
    at = lambda off: from_ring((place + off + rep_count) % rep_count)
    steps = partners(ep_count)
    full_hops = (rep_count - 1) // 2
    last_hop = rep_count // 2
    half = unit_cols // 2 // 128 * 128
    parts = {1: pl.ds(0, half), -1: pl.ds(half, unit_cols - half)}

    def piece_for(dest):
        start = pl.multiple_of((dest % group) * unit_cols, 128)
        return hidden_ref.at[dest // group, :, pl.ds(start, unit_cols)]

    def grad_cols(owner):
        return grad_ref.at[:, pl.ds(pl.multiple_of(owner * col_width, 128), col_width)]

    def remote(src, dst, send, recv, to_rep, to_ep):
        return pltpu.make_async_remote_copy(
            src_ref=src, dst_ref=dst, send_sem=send, recv_sem=recv,
            device_id=(to_rep, to_ep), device_id_type=MESH,
        )

    def hop(i, way, distance):
        source = steps[i][1](ep)
        origin = at(-way * (distance - 1))
        src = dst = rows_ref.at[origin, source]
        if distance == 1 and i == 0:
            src = piece_for(ep)
        if distance > full_hops:
            src, dst = src.at[:, parts[way]], dst.at[:, parts[way]]
        lane = (0 if way == 1 else 1, distance - 1, i)
        return remote(src, dst, ring_send.at[lane], ring_recv.at[lane], at(way), ep)

    hops = {}

    def start_hop(i, distance):
        if distance > last_hop:
            return
        for way in (1, -1):
            hops[i, way, distance] = hop(i, way, distance)
            hops[i, way, distance].start()

    near = []
    for r in range(1, rep_count):
        near.append(remote(route_ref, routes.at[rep], route_send.at[r], route_recv.at[r], at(r), ep))
        near.append(remote(grad_cols(at(r)), grads.at[rep], grad_send.at[r], grad_recv.at[r], at(r), ep))
    exchanges = [None]
    for i in range(1, ep_count):
        dest = steps[i][0](ep)
        exchanges.append(
            remote(piece_for(dest), rows_ref.at[rep, ep], send_sem.at[i], recv_sem.at[i], rep, dest)
        )
    own = [
        pltpu.make_async_copy(route_ref, routes.at[rep], own_sem.at[0]),
        pltpu.make_async_copy(grad_cols(rep), grads.at[rep], own_sem.at[1]),
        pltpu.make_async_copy(piece_for(ep), rows_ref.at[rep, ep], own_sem.at[2]),
    ]

    def pack(r):
        tok_count = grads.shape[1]
        lanes = routes.shape[2]
        route = routes[r].astype(jnp.float32)
        weight, named = route[:EXPERTS], route[EXPERTS:]
        before = (
            lax.broadcasted_iota(jnp.int32, (lanes, lanes), 0)
            < lax.broadcasted_iota(jnp.int32, (lanes, lanes), 1)
        ).astype(jnp.float32).astype(jnp.bfloat16)
        row = jnp.dot(named.astype(jnp.bfloat16), before, preferred_element_type=jnp.float32)
        row = jnp.where(named > 0.5, row, -1.0)
        slots = lax.broadcasted_iota(jnp.int32, (CAP, lanes), 0).astype(jnp.float32)
        picks = jnp.concatenate(
            [jnp.where(row[e : e + 1] == slots, weight[e : e + 1], 0.0) for e in range(EXPERTS)], axis=0
        ).astype(jnp.bfloat16)
        scaled = jnp.dot(picks[:, :tok_count], grads[r], preferred_element_type=jnp.float32)
        for e in range(EXPERTS):
            packed[r, e] = scaled[e * CAP : (e + 1) * CAP].astype(jnp.bfloat16)

    for copy in near:
        copy.start()
    exchanges[1].start()
    start_hop(0, 1)
    for copy in exchanges[2:]:
        copy.start()
    for copy in own:
        copy.start()
    spread = []
    for i in range(1, ep_count + last_hop):
        if i < ep_count:
            exchanges[i].wait_recv()
            start_hop(i, 1)
        if i == 1:
            for copy in near:
                copy.wait()
            for copy in own:
                copy.wait()
            for r in range(rep_count):
                pack(r)
        for distance in range(1, last_hop + 1):
            j = i - distance
            if 0 <= j < ep_count:
                for way in (1, -1):
                    hops[j, way, distance].wait_recv()
                start_hop(j, distance + 1)
        if i == 1:
            spread.append(
                pltpu.make_async_copy(packed.at[:, ep // group], cols_ref.at[:, ep], own_sem.at[3])
            )
            for k in range(1, ep_count):
                dest = steps[k][0](ep)
                spread.append(
                    remote(
                        packed.at[:, dest // group], cols_ref.at[:, ep],
                        cols_send.at[k], cols_recv.at[k], rep, dest,
                    )
                )
            for copy in spread:
                copy.start()
    for copy in spread:
        copy.wait()
    for copy in exchanges[1:]:
        copy.wait_send()
    for copy in hops.values():
        copy.wait_send()


def exchange(hidden, grad, route, rep_count, ep_count):
    unit_cols = hidden.shape[2] * EXPERTS // ep_count
    tok_count = grad.shape[0]
    col_width = grad.shape[1] // rep_count
    hops = max(1, rep_count // 2)
    dma = pltpu.SemaphoreType.DMA
    return pl.pallas_call(
        functools.partial(exchange_kernel, rep_count, ep_count),
        out_shape=(
            jax.ShapeDtypeStruct((rep_count, ep_count, CAP, unit_cols), jnp.bfloat16),
            jax.ShapeDtypeStruct((rep_count, ep_count, CAP, col_width), jnp.bfloat16),
        ),
        in_specs=[pl.BlockSpec(memory_space=pl.ANY)] * 3,
        out_specs=(pl.BlockSpec(memory_space=pl.ANY),) * 2,
        scratch_shapes=[
            pltpu.VMEM((rep_count, tok_count, col_width), jnp.bfloat16),
            pltpu.VMEM((rep_count,) + route.shape, jnp.bfloat16),
            pltpu.VMEM((rep_count, EXPERTS, CAP, col_width), jnp.bfloat16),
            dma((4,)),
            dma((ep_count,)),
            dma((ep_count,)),
            dma((2, hops, ep_count)),
            dma((2, hops, ep_count)),
            dma((rep_count,)),
            dma((rep_count,)),
            dma((rep_count,)),
            dma((rep_count,)),
            dma((ep_count,)),
            dma((ep_count,)),
        ],
        compiler_params=pltpu.CompilerParams(
            has_side_effects=True, vmem_limit_bytes=4 * 1024 * 1024
        ),
    )(hidden, grad, route)


def per_device(out_grad, saved_hidden, combine, expert_ids):
    ep_count = lax.axis_size("ep")
    rep_count = lax.axis_size("rep")
    tok_count, model_width = out_grad.shape
    units = saved_hidden.shape[2]
    lanes = -(-tok_count // 128) * 128
    ids, probs = expert_ids.T, combine.T
    experts = jnp.arange(EXPERTS, dtype=jnp.int32)
    chosen = ids[:, None, :] == experts[None, :, None]
    named = jnp.any(chosen, axis=0)
    weight = jnp.sum(jnp.where(chosen, probs[:, None, :].astype(jnp.float32), jnp.float32(0.0)), axis=0)
    route = jnp.concatenate([weight, named.astype(jnp.float32)], axis=0).astype(jnp.bfloat16)
    route = jnp.pad(route, ((0, 0), (0, lanes - tok_count)))
    before = jnp.arange(tok_count)[:, None] < jnp.arange(tok_count)[None, :]
    row = jnp.dot(
        named.astype(jnp.bfloat16), before.astype(jnp.bfloat16), preferred_element_type=jnp.float32
    )
    slots = jnp.arange(CAP, dtype=jnp.float32)
    at_slot = row[:, None, None, :] == slots[None, :, None, None]
    pick = (at_slot & chosen.transpose(1, 0, 2)[:, None]).astype(jnp.bfloat16)
    send_hidden = lax.dot_general(
        pick.reshape(EXPERTS * CAP, TOP, tok_count),
        saved_hidden,
        (((1, 2), (1, 0)), ((), ())),
        preferred_element_type=jnp.float32,
    ).astype(jnp.bfloat16)
    rows, cols = exchange(
        send_hidden.reshape(EXPERTS, CAP, units), out_grad, route, rep_count, ep_count
    )
    row_total = rep_count * ep_count * CAP
    return lax.dot_general(
        rows.reshape(row_total, rows.shape[3]),
        cols.reshape(row_total, cols.shape[3]),
        (((0,), (0,)), ((), ())),
        preferred_element_type=jnp.float32,
    )


def solution(mesh):
    in_specs = (
        P(("rep", "ep"), None),
        P(("rep", "ep"), None, None),
        P(("rep", "ep"), None),
        P(("rep", "ep"), None),
    )
    out_specs = P("ep", "rep")
    return jax.shard_map(
        per_device, mesh=mesh, in_specs=in_specs, out_specs=out_specs, check_vma=False
    )
```

time: 125 us -> 118 us (0.944)
  Pallas kernels: 110 us -> 104 us
  matrix products: 11.8 us -> 10.5 us
    pallas_call x1, Pallas kernels: 110 us -> 104 us  [exchange(): pl.pallas_call(functools.partial(exchange_kernel, rep_count, ep_count), o...]
    dot_general x2, matrix products: 2.34 us -> 1.05 us  [the longest x1 0.93 us: per_device(): lax.dot_general(pick.reshape(EXPERTS * CAP, TOP, tok_count), saved_hidden...]
where the time goes in v3:
time: 118 us
  Pallas kernels  104 us (88%)
  matrix products  10.5 us (9%)
  other arithmetic  2.99 us (3%)
    pallas_call x1, Pallas kernels, exchange(): pl.pallas_call(functools.partial(exchange_kernel, rep_count, ep_count), o...  104 us
    dot_general x1, matrix products, per_device(): lax.dot_general(rows.reshape(row_total, rows.shape[3]), cols.reshape(row_...  9.45 us

profile of v3, /device:TPU:8, one launch (start us, length us, event | category | flops | bytes accessed | tf_op | source)
XLA Modules:
  0.0 118.1 jit_solution(15556550974419083730)
XLA Ops:
  0.0 0.0 copy-start
  0.0 0.8 fusion.5
  0.8 0.7 convert_bitcast_fusion
  1.5 0.7 select_reduce_fusion
  2.2 0.7 iota_compare_fusion.3
  2.9 0.1 fusion.2
  3.0 0.1 eq.54
  3.1 0.1 bitcast_compare_fusion
  3.2 0.0 copy-done
  3.2 0.9 fusion
  4.2 0.0 copy-start.1
  4.2 0.9 copy-done.1
  5.1 103.5 %shard_map.46 = (bf16[4,8,24,7168]{3,2,1,0:T(8,128)(2,1)S(1)}, bf16[4,8,24,512]{3,2,1,0:T(8,128)(2,1)S(1)}) custom-call(bf16[8,24,7168]{2,1,0:T(8,128)(2,1)S(1)} %bitcast.20, bf16[64,2048]{1,0:T(8,128)(2,1)S(1)} %copy-done.1, bf16[16,128]{1,0:T(8,128)(2,1)S(1)} %fusion.6.route_ref), custom_call_target="tpu_custom_call" | custom-call | tf_op jit(solution)/shard_map/pallas_call | solution.py:184
  108.7 9.5 %convolution_bitcast_fusion = f32[7168,512]{1,0:T(8,128)} fusion(bf16[4,8,24,7168]{3,2,1,0:T(8,128)(2,1)S(1)} %get-tuple-element.7, bf16[4,8,24,512]{3,2,1,0:T(8,128)(2,1)S(1)} %get-tuple-element.8), kind=kOutput, calls=%fused_computation | convolution fusion | flops 5637144576 | bytes 26476544 | tf_op jit(solution)/shard_map/dot_general | solution.py:244
  (4 shorter events, 0.1 us)
Async XLA Ops:
  0.0 3.2 %copy-start = (bf16[64,2,7168]{2,1,0:T(2,128)(2,1)S(1)}, bf16[64,2,7168]{2,1,0:T(2,128)(2,1)}, u32[]{:S(2)}) copy-start(bf16[64,2,7168]{2,1,0:T(2,128)(2,1)} %param.5) | copy-start | bytes 5505028
  4.2 1.0 copy-start.1

commit v4 on v3

--- a/solution.py
+++ b/solution.py
@@ -153,7 +153,7 @@
                 for way in (1, -1):
                     hops[j, way, distance].wait_recv()
                 start_hop(j, distance + 1)
-        if i == 1:
+        if i == ep_count // 2 + 1:
             spread.append(
                 pltpu.make_async_copy(packed.at[:, ep // group], cols_ref.at[:, ep], own_sem.at[3])
             )
@@ -187,7 +187,11 @@
             jax.ShapeDtypeStruct((rep_count, ep_count, CAP, unit_cols), jnp.bfloat16),
             jax.ShapeDtypeStruct((rep_count, ep_count, CAP, col_width), jnp.bfloat16),
         ),
-        in_specs=[pl.BlockSpec(memory_space=pl.ANY)] * 3,
+        in_specs=[
+            pl.BlockSpec(memory_space=pl.ANY),
+            pl.BlockSpec(memory_space=pltpu.HBM),
+            pl.BlockSpec(memory_space=pl.ANY),
+        ],
         out_specs=(pl.BlockSpec(memory_space=pl.ANY),) * 2,
         scratch_shapes=[
             pltpu.VMEM((rep_count, tok_count, col_width), jnp.bfloat16),
@@ -217,11 +221,14 @@
     tok_count, model_width = out_grad.shape
     units = saved_hidden.shape[2]
     lanes = -(-tok_count // 128) * 128
-    ids, probs = expert_ids.T, combine.T
-    experts = jnp.arange(EXPERTS, dtype=jnp.int32)
+    small = lax.optimization_barrier(
+        jnp.concatenate([expert_ids.T.astype(jnp.float32), combine.T.astype(jnp.float32)], axis=0)
+    )
+    ids, probs = small[:TOP], small[TOP:]
+    experts = jnp.arange(EXPERTS, dtype=jnp.int32).astype(jnp.float32)
     chosen = ids[:, None, :] == experts[None, :, None]
     named = jnp.any(chosen, axis=0)
-    weight = jnp.sum(jnp.where(chosen, probs[:, None, :].astype(jnp.float32), jnp.float32(0.0)), axis=0)
+    weight = jnp.sum(jnp.where(chosen, probs[:, None, :], jnp.float32(0.0)), axis=0)
     route = jnp.concatenate([weight, named.astype(jnp.float32)], axis=0).astype(jnp.bfloat16)
     route = jnp.pad(route, ((0, 0), (0, lanes - tok_count)))
     before = jnp.arange(tok_count)[:, None] < jnp.arange(tok_count)[None, :]

time: 118 us -> 117 us (level)
  no operation moved by 1% of the time
where the time goes in v4:
time: 117 us
  Pallas kernels  104 us (89%)
  matrix products  10.5 us (9%)
  other arithmetic  1.85 us (2%)
    pallas_call x1, Pallas kernels, exchange(): pl.pallas_call(functools.partial(exchange_kernel, rep_count, ep_count), o...  104 us
    dot_general x1, matrix products, per_device(): lax.dot_general(rows.reshape(row_total, rows.shape[3]), cols.reshape(row_...  9.45 us

profile of v4, /device:TPU:8, one launch (start us, length us, event | category | flops | bytes accessed | tf_op | source)
XLA Modules:
  0.0 117.0 jit_solution(748474091447274277)
XLA Ops:
  0.0 0.0 copy-start
  0.0 0.8 convert_bitcast_fusion
  0.8 0.7 convert_bitcast_fusion.1
  1.5 0.1 compare_reduce_fusion
  1.6 0.1 fusion.3
  1.6 0.1 broadcast_compare_fusion
  1.7 0.1 fusion.2
  1.9 0.1 eq.54
  2.0 0.1 bitcast_compare_fusion
  2.1 0.0 copy-done
  2.1 0.9 fusion
  3.0 0.0 copy-start.1
  3.1 0.9 copy-done.1
  4.0 103.5 %shard_map.46 = (bf16[4,8,24,7168]{3,2,1,0:T(8,128)(2,1)S(1)}, bf16[4,8,24,512]{3,2,1,0:T(8,128)(2,1)S(1)}) custom-call(bf16[8,24,7168]{2,1,0:T(8,128)(2,1)S(1)} %bitcast.21, bf16[64,2048]{1,0:T(8,128)(2,1)S(1)} %copy-done.1, bf16[16,128]{1,0:T(8,128)(2,1)S(1)} %fusion.6.route_ref), custom_call_target="tpu_custom_call" | custom-call | tf_op jit(solution)/shard_map/pallas_call | solution.py:184
  107.5 9.4 %convolution_bitcast_fusion = f32[7168,512]{1,0:T(8,128)} fusion(bf16[4,8,24,7168]{3,2,1,0:T(8,128)(2,1)S(1)} %get-tuple-element.7, bf16[4,8,24,512]{3,2,1,0:T(8,128)(2,1)S(1)} %get-tuple-element.8), kind=kOutput, calls=%fused_computation | convolution fusion | flops 5637144576 | bytes 26476544 | tf_op jit(solution)/shard_map/dot_general | solution.py:251
  (7 shorter events, 0.1 us)
Async XLA Ops:
  0.0 2.1 %copy-start = (bf16[64,2,7168]{2,1,0:T(2,128)(2,1)S(1)}, bf16[64,2,7168]{2,1,0:T(2,128)(2,1)}, u32[]{:S(2)}) copy-start(bf16[64,2,7168]{2,1,0:T(2,128)(2,1)} %param.5) | copy-start | bytes 5505028
  3.0 1.0 copy-start.1
